TPU v7x, 256 devices: a whole 4x4x8 slice. The times are simulated.
256 devices in a mesh: dp: 64 (over z, x_hi, y), rep: 4 (over x_lo, core).
Axes of the slice: x: 4 (x_hi: 2, x_lo: 2; x = x_hi * 2 + x_lo), y: 4, z: 8, core: 2. Of those that a mesh axis runs over, the one named last changes fastest.
Arguments:
- tokens: bfloat16 [1024, 128, 2048], P(('dp', 'rep')), may hold values from -32 to 32, as said below
- cotangent: bfloat16 [1024, 128, 1024], P(('dp', 'rep')), may hold values from -6 to 6
- projection: bfloat16 [2048, 1536], replicated, may hold values from -0.25 to 0.25
- block_lengths: int32 [256, 4], P(('dp', 'rep')), may hold values from 0 to 128, as said below
- destination: int32 [256], P(('dp', 'rep')), may hold values from -1 to 63, as said below
Outputs:
- direction: float32 [2048, 1536], P(('dp', 'rep'))
Inputs may be any that keep to these rules, and one draw needn't show every extreme that they name: `tokens`: clipped at the range's ends. `block_lengths`: A device's live slots come first, all of length 128 except the last live one, which holds 64 to 128 tokens; later slots have length 0. A device has 1 to 4 live slots, and some device has 4 in every draw. A device has a destination exactly when it has 4 live slots. The destination's dp index differs from the sender's in exactly one bit, the rep index is the same, the receiver has at most 2 live slots, and no device receives from two senders.
All inputs are finite; a program needn't handle non-finite values.
Results may differ from a plain program's by a relative error of at most 0.006.
The roundings to bfloat16 on the way count: a program that leaves them out, or rounds other values in their place, can miss the bound.
Values may be sent and summed in bfloat16 or wider, within the bound.
A program may use at most 128 MiB of HBM per device.

v0:
```python
import math

import jax
import jax.numpy as jnp
from jax import lax
from jax.experimental import pallas as pl
from jax.experimental.pallas import tpu as pltpu
from jax.sharding import Mesh
from jax.sharding import PartitionSpec as P

HS = 256
HEADS = 4
BLOCK = 128
DP_REP = ("dp_0", "dp_1", "dp_2", "rep_0", "rep_1")
REP = ("rep_0", "rep_1")
DP = ("dp_0", "dp_1", "dp_2")
GROUPS = HEADS + 2
D = 2048
MESH = pl.DeviceIdType.MESH
F32 = jnp.float32
BF16 = jnp.bfloat16


def dot(a, b, ca, cb):
    return lax.dot_general(a, b, (((ca,), (cb,)), ((), ())), preferred_element_type=F32)


def gradient_kernel(
    lengths, info, tok, cot, tok_a, cot_a, tok_b, cot_b, proj, soft, x, up, joined, comb, xt, grad
):
    rows = 3 * BLOCK
    way = info[1, 0]

    def chosen(own, a, b):
        return jnp.where(way == 1, a, jnp.where(way == 2, b, own))

    x[0 : 2 * BLOCK, :] = tok[0:2].reshape(2 * BLOCK, D)
    x[2 * BLOCK : rows, :] = chosen(tok[2], tok_a[...], tok_b[...])
    up[0 : 2 * BLOCK, :] = cot[0:2].reshape(2 * BLOCK, HEADS * HS)
    up[2 * BLOCK : rows, :] = chosen(cot[2], cot_a[...], cot_b[...])

    @pl.loop(0, GROUPS)
    def _(g):
        cols = pl.ds(pl.multiple_of(g * HS, HS), HS)
        joined[:, cols] = dot(x[...], proj[:, cols], 1, 0).astype(BF16)

    @pl.loop(0, D // 256)
    def _(r):
        at = pl.ds(pl.multiple_of(r * 256, 256), 256)
        xt[at, :] = x[:, at].T

    scale = HS ** (-0.5)

    @pl.loop(0, 3)
    def _(b):
        at = pl.ds(pl.multiple_of(b * BLOCK, BLOCK), BLOCK)
        length = jnp.where(b == 2, info[2, 0], lengths[b])

        def heads(ref):
            return jnp.concatenate(
                [ref[at, h * HS : (h + 1) * HS] for h in range(HEADS)], axis=0
            )

        query = heads(joined)
        keys = joined[at, HEADS * HS : (HEADS + 1) * HS]
        values = joined[at, (HEADS + 1) * HS :]
        shape = (HEADS * BLOCK, BLOCK)
        row = lax.rem(lax.broadcasted_iota(jnp.int32, shape, 0), BLOCK)
        col = lax.broadcasted_iota(jnp.int32, shape, 1)
        allowed = (col <= row) & (col < length)
        scores = jnp.where(allowed, dot(query, keys, 1, 1) * scale, -1e30)
        peak = jnp.max(scores, axis=-1, keepdims=True)
        expo = jnp.exp(scores - peak)
        weights = expo / jnp.sum(expo, axis=-1, keepdims=True)
        wide = (HEADS * BLOCK, HS)
        live = lax.rem(lax.broadcasted_iota(jnp.int32, wide, 0), BLOCK) < length
        upstream = jnp.where(live, heads(up).astype(F32), 0.0).astype(BF16)
        probs = weights.astype(BF16)
        grad_values = dot(probs.T, upstream, 1, 0).astype(BF16)
        grad_probs = dot(upstream, values, 1, 1)
        centre = jnp.sum(weights * grad_probs, axis=-1, keepdims=True)
        grad_scores = (weights * (grad_probs - centre) * scale).astype(BF16)
        grad_query = dot(grad_scores, keys, 1, 0).astype(BF16)
        grad_keys = dot(grad_scores.T, query, 1, 0).astype(BF16)
        for h in range(HEADS):
            comb[at, h * HS : (h + 1) * HS] = grad_query[h * BLOCK : (h + 1) * BLOCK]
        comb[at, HEADS * HS : (HEADS + 1) * HS] = grad_keys
        comb[at, (HEADS + 1) * HS :] = grad_values

    tile = 256

    @pl.loop(0, GROUPS)
    def _(g):
        cols = pl.ds(pl.multiple_of(g * HS, HS), HS)
        total = jnp.zeros((8, HS), F32)
        for r in range(D // tile):
            part = dot(xt[r * tile : (r + 1) * tile, :], comb[:, cols], 1, 0)
            grad[r * tile : (r + 1) * tile, :] = part
            total += jnp.sum((part * part).reshape(tile // 8, 8, HS), axis=0)
        total = jnp.sum(jnp.sum(total, axis=0, keepdims=True), axis=1, keepdims=True)
        spread = 0.25 * jnp.sqrt(total * (1.0 / (D * HS)) + 1e-06)

        @pl.loop(0, D // 128)
        def _(r):
            at = pl.ds(pl.multiple_of(r * 128, 128), 128)
            part = grad[at, :]
            soft[g, at, :] = (part / (jnp.abs(part) + spread)).astype(BF16)


def soft_signs(lengths, info, tokens, cotangent, moved, projection):
    vmem = pltpu.VMEM
    rows = 3 * BLOCK
    width = GROUPS * HS
    return pl.pallas_call(
        gradient_kernel,
        out_shape=jax.ShapeDtypeStruct((GROUPS, D, HS), BF16),
        grid=(1,),
        in_specs=[
            pl.BlockSpec(memory_space=pltpu.SMEM),
            pl.BlockSpec(memory_space=pltpu.SMEM),
            pl.BlockSpec((3, BLOCK, D), lambda i: (0, 0, 0)),
            pl.BlockSpec((3, BLOCK, HEADS * HS), lambda i: (0, 0, 0)),
            pl.BlockSpec((BLOCK, D), lambda i: (0, 0)),
            pl.BlockSpec((BLOCK, HEADS * HS), lambda i: (0, 0)),
            pl.BlockSpec((BLOCK, D), lambda i: (0, 0)),
            pl.BlockSpec((BLOCK, HEADS * HS), lambda i: (0, 0)),
            pl.BlockSpec((D, width), lambda i: (0, 0)),
        ],
        out_specs=pl.BlockSpec((GROUPS, D, HS), lambda i: (0, 0, 0)),
        scratch_shapes=[
            vmem((rows, D), BF16),
            vmem((rows, HEADS * HS), BF16),
            vmem((rows, width), BF16),
            vmem((rows, width), BF16),
            vmem((D, rows), BF16),
            vmem((D, HS), F32),
        ],
        compiler_params=pltpu.CompilerParams(vmem_limit_bytes=60 << 20),
        name="soft_signs",
    )(lengths, info, tokens, cotangent, *moved, projection)


NZ, NY, NX = 8, 4, 4


def wrap(i, n):
    return lax.rem(i + n, n)


def vote_kernel(soft, out, own, part, wz, wx, wy, rzp0, rzp1, rzm0, rzm1, szp0, szp1, szm0,
                szm1, rx, sx, ry, sy, ux, uy, uz, vx, vy, vz, tx, ty, tz, qx, qy, qz, res, fin,
                loc, s0, r0, s1, r1, s2, r2, s3, r3, s4, r4):
    z, xh, y, xl, core = [lax.axis_index(a) for a in DP_REP]
    x = xh * 2 + xl

    def at_x(i):
        return {"dp_1": lax.div(i, 2), "rep_0": lax.rem(i, 2)}

    def at_y(i):
        return {"dp_2": i}

    def at_z(i):
        return {"dp_0": i}

    partner = {"rep_1": 1 - core}

    barrier = pltpu.get_barrier_semaphore()
    peers = [partner]
    peers += [at_x(wrap(x + d, NX)) for d in range(1, NX)]
    peers += [at_y(wrap(y + d, NY)) for d in range(1, NY)]
    peers += [at_z(wrap(z + d, NZ)) for d in range(1, NZ)]
    for j in range(3):
        pltpu.make_async_copy(soft.at[core * 3 + j], own.at[j], loc.at[j]).start()
    for peer in peers:
        pl.semaphore_signal(barrier, inc=1, device_id=peer, device_id_type=MESH)
    pl.semaphore_wait(barrier, len(peers))

    sent = []

    def send(src, dst, ss, rs, dev):
        copy = pltpu.make_async_remote_copy(
            src_ref=src, dst_ref=dst, send_sem=ss, recv_sem=rs, device_id=dev, device_id_type=MESH
        )
        copy.start()
        sent.append(copy)
        return copy

    first = [
        send(soft.at[(1 - core) * 3 + j], part.at[j], s0.at[j], r0.at[j], partner)
        for j in range(3)
    ]

    def add(*refs):
        total = refs[0][...].astype(F32)
        for ref in refs[1:]:
            total = total + ref[...].astype(F32)
        return total

    def arrive(j):
        pltpu.make_async_copy(soft.at[core * 3 + j], own.at[j], loc.at[j]).wait()
        first[j].wait_recv()

    arrive(0)

    @pl.loop(0, NZ)
    def _(a):
        for h in range(2):
            wz[a, h] = add(own.at[0, a, h], part.at[0, a, h]).astype(BF16)

    up_z, down_z = at_z(wrap(z + 1, NZ)), at_z(wrap(z - 1, NZ))

    def zpiece(d, h):
        return wz.at[wrap(z + d, NZ), h]

    zp0 = [send(zpiece(4, 0), rzp0.at[0], s1.at[0], r1.at[0], up_z)]
    zm1 = [send(zpiece(-4, 1), rzm1.at[0], s1.at[1], r1.at[1], down_z)]
    zp1 = [send(zpiece(3, 1), rzp1.at[0], s1.at[2], r1.at[2], up_z)]
    zm0 = [send(zpiece(-3, 0), rzm0.at[0], s1.at[3], r1.at[3], down_z)]

    def four_ring(j, c, w, dev, recv, base):
        ahead, behind = dev(wrap(c + 1, 4)), dev(wrap(c - 1, 4))
        far = wrap(c + 2, 4)
        lo, hi = pl.ds(0, 4), pl.ds(4, 4)
        sem = lambda i: (s2.at[base + i], r2.at[base + i])
        return [
            send(w(far).at[lo], recv.at[0], *sem(0), ahead),
            send(w(far).at[hi], recv.at[1], *sem(1), behind),
            send(w(wrap(c + 1, 4)).at[hi], recv.at[3], *sem(2), ahead),
            send(w(wrap(c - 1, 4)).at[lo], recv.at[4], *sem(3), behind),
        ]

    def relay(c, w, dev, recv, hold, base, begun):
        ahead, behind = dev(wrap(c + 1, 4)), dev(wrap(c - 1, 4))
        sem = lambda i: (s2.at[base + i], r2.at[base + i])
        out_copies = []
        for i, (step, half, slot, to) in enumerate(((1, 0, 2, ahead), (-1, 4, 5, behind))):
            begun[i].wait_recv()
            mine = w(wrap(c + step, 4))

            @pl.loop(0, 4)
            def _(a):
                hold[i, a] = add(mine.at[half + a], recv.at[i, a]).astype(BF16)

            out_copies.append(send(hold.at[i], recv.at[slot], *sem(4 + i), to))
        return out_copies

    wx_of = lambda c: wx.at[lax.div(c, 2), lax.rem(c, 2)]
    wy_of = lambda c: wy.at[c]

    arrive(1)

    @pl.loop(0, NZ)
    def _(a):
        for h in range(2):
            for l in range(2):
                wx[h, l, a] = add(own.at[1, a, h, :, l], part.at[1, a, h, :, l]).astype(BF16)

    bx = four_ring(1, x, wx_of, at_x, rx, 0)
    arrive(2)

    @pl.loop(0, NZ)
    def _(a):
        for b in range(NY):
            wy[b, a] = add(own.at[2, a, :, b], part.at[2, a, :, b]).astype(BF16)

    by = four_ring(2, y, wy_of, at_y, ry, 6)

    def z_relay(k):
        def hop(chain, recv, hold, d, h, sem, to):
            chain[k - 1].wait_recv()
            hold[k - 1] = add(zpiece(d, h), recv.at[k - 1]).astype(BF16)
            chain.append(send(hold.at[k - 1], recv.at[k], s1.at[sem], r1.at[sem], to))

        hop(zp0, rzp0, szp0, 4 - k, 0, 4 * k, up_z)
        hop(zm1, rzm1, szm1, k - 4, 1, 4 * k + 1, down_z)
        if k < 3:
            hop(zp1, rzp1, szp1, 3 - k, 1, 4 * k + 2, up_z)
            hop(zm0, rzm0, szm0, k - 3, 0, 4 * k + 3, down_z)

    z_relay(1)
    cx = relay(x, wx_of, at_x, rx, sx, 0, bx)
    cy = relay(y, wy_of, at_y, ry, sy, 6, by)
    z_relay(2)
    z_relay(3)

    def settle(c, w, recv, begun, later, store):
        later[0].wait_recv()
        begun[2].wait_recv()
        begun[3].wait_recv()
        later[1].wait_recv()
        mine = w(c)

        @pl.loop(0, 4)
        def _(a):
            store(a, add(mine.at[a], recv.at[2, a], recv.at[4, a]))
            store(4 + a, add(mine.at[4 + a], recv.at[3, a], recv.at[5, a]))

    def store_x(a, v):
        ux[:, a] = v.astype(BF16)

    def store_y(a, v):
        uy[:, :, a] = v.astype(BF16)

    def spread(u, c, n, dev, recv, ss, rs, base):
        return [
            send(u(wrap(c + d, n)), recv.at[d - 1], ss.at[base + d - 1], rs.at[base + d - 1],
                 dev(wrap(c + d, n)))
            for d in range(1, n)
        ]

    ux_of = lambda c: ux.at[c]
    uy_of = lambda c: uy.at[lax.div(c, 2), lax.rem(c, 2)]
    uz_of = lambda c: uz.at[lax.div(c, 2), lax.rem(c, 2)]
    settle(x, wx_of, rx, bx, cx, store_x)
    dx = spread(ux_of, y, NY, at_y, vx, s3, r3, 0)
    settle(y, wy_of, ry, by, cy, store_y)
    dy = spread(uy_of, x, NX, at_x, vy, s3, r3, 3)
    for chain in (zp0, zm0, zp1, zm1):
        chain[-1].wait_recv()
    for h, (a, b) in enumerate(((rzp0.at[3], rzm0.at[2]), (rzp1.at[2], rzm1.at[3]))):
        v = add(zpiece(0, h), a, b)
        for l in range(2):
            uz[h, l] = v[:, l].astype(BF16)
    dz = spread(uz_of, x, NX, at_x, vz, s3, r3, 6)

    def gather(copies, u, c, recv, hold):
        for copy in copies:
            copy.wait_recv()
        hold[...] = add(u(c), *[recv.at[i] for i in range(len(copies))]).astype(BF16)

    gather(dx, ux_of, y, vx, tx)
    ex = spread(lambda c: tx.at[c], z, NZ, at_z, qx, s4, r4, 0)
    gather(dy, uy_of, x, vy, ty)
    ey = spread(lambda c: ty.at[c], z, NZ, at_z, qy, s4, r4, 7)
    gather(dz, uz_of, x, vz, tz)
    ez = spread(lambda c: tz.at[c], y, NY, at_y, qz, s4, r4, 14)

    def finish(j, copies, mine, recv):
        for copy in copies:
            copy.wait_recv()
        total = add(mine, *[recv.at[i] for i in range(len(copies))]) * (1.0 / 16.0)
        res[j, 0] = total[0:8]
        res[j, 1] = total[8:16]

    finish(0, ez, tz.at[y], qz)
    finish(1, ex, tx.at[z], qx)
    finish(2, ey, ty.at[z], qy)
    ends = [
        send(res.at[j, 1 - core], fin.at[j], s0.at[3 + j], r0.at[3 + j], partner) for j in range(3)
    ]
    for j in range(3):
        out[core * 3 + j] = res[j, core]
    for j in range(3):
        ends[j].wait_recv()
        out[(1 - core) * 3 + j] = fin[j]
    for copy in sent:
        copy.wait_send()


def vote_sum(soft):
    vmem = pltpu.VMEM
    t = (16, HS)
    bf = lambda *dims: vmem(dims + t, BF16)
    sems = lambda n: pltpu.SemaphoreType.DMA((n,))
    scratch = [
        bf(3, 8, 2, 4, 2),
        bf(3, 8, 2, 4, 2),
        bf(8, 2, 4, 2),
        bf(2, 2, 8, 4),
        bf(4, 8, 2, 2),
        bf(4, 4, 2), bf(3, 4, 2), bf(3, 4, 2), bf(4, 4, 2),
        bf(3, 4, 2), bf(2, 4, 2), bf(2, 4, 2), bf(3, 4, 2),
        bf(6, 4, 4), bf(2, 4, 4),
        bf(6, 4, 2, 2), bf(2, 4, 2, 2),
        bf(4, 8), bf(2, 2, 8), bf(2, 2, 4),
        bf(3, 8), bf(3, 8), bf(3, 4),
        bf(8), bf(8), bf(4),
        bf(7), bf(7), bf(3),
        vmem((3, 2, 8, HS), F32),
        vmem((3, 8, HS), F32),
        sems(3),
        sems(6), sems(6), sems(16), sems(16), sems(12), sems(12), sems(9), sems(9), sems(17), sems(17),
    ]
    return pl.pallas_call(
        vote_kernel,
        out_shape=jax.ShapeDtypeStruct((GROUPS, 8, HS), F32),
        in_specs=[pl.BlockSpec(memory_space=pl.ANY)],
        out_specs=pl.BlockSpec(memory_space=pltpu.VMEM),
        scratch_shapes=scratch,
        compiler_params=pltpu.CompilerParams(
            collective_id=1, has_side_effects=True, vmem_limit_bytes=40 << 20
        ),
        name="vote_sum",
    )(soft)


LEVELS = 6
PAIRS = [(a, b) for a in range(LEVELS) for b in range(a + 1, LEVELS)]
ALONE = {0: (0, 2), 1: (1, 2), 2: (0, 2), 3: (2, 3), 4: (2, 4), 5: (2, 5)}


def flipped(i, m):
    return i + m - 2 * m * lax.rem(lax.div(i, m), 2)


def across(level):
    if level < 2:
        return {"dp_2": flipped(lax.axis_index("dp_2"), 1 << level)}
    if level == 2:
        return {"dp_1": 1 - lax.axis_index("dp_1")}
    return {"dp_0": flipped(lax.axis_index("dp_0"), 1 << (level - 3))}


def plan_kernel(dest, lengths, info, tile, from_x, from_y, from_z, ss, rs):
    z, xh, y, xl, core = [lax.axis_index(a) for a in DP_REP]
    x = xh * 2 + xl
    rank = (z * 2 + xh) * 4 + y
    pair = xl * 2 + core

    def at_x(i, c):
        return {"dp_1": lax.div(i, 2), "rep_0": lax.rem(i, 2), "rep_1": c}

    stage_x = [{"rep_1": 1 - core}]
    stage_x += [at_x(wrap(x + d, NX), core) for d in range(1, NX)]
    stage_x += [at_x(wrap(x + d, NX), 1 - core) for d in range(1, NX)]
    stage_y = [{"dp_2": wrap(y + d, NY)} for d in range(1, NY)]
    stage_z = [{"dp_0": wrap(z + d, NZ)} for d in range(1, NZ)]
    peers = stage_x + stage_y + stage_z
    barrier = pltpu.get_barrier_semaphore()
    for peer in peers:
        pl.semaphore_signal(barrier, inc=1, device_id=peer, device_id_type=MESH)

    shape = (8, 128)
    slot = lax.broadcasted_iota(jnp.int32, shape, 0) * 128 + lax.broadcasted_iota(jnp.int32, shape, 1)
    target = jnp.full(shape, dest[0], jnp.int32)
    code = jnp.zeros(shape, jnp.int32)
    for level in range(LEVELS):
        code = jnp.where(target == flipped(rank, 1 << level), level + 1, code)
    code = code * 256 + jnp.full(shape, lengths[3], jnp.int32)
    mine = (slot == rank * 4 + pair) & (target >= 0)
    tile[0] = jnp.where(mine, code, 0)
    pl.semaphore_wait(barrier, len(peers))

    sent = []
    base = 0
    for k, (stage, landing) in enumerate(((stage_x, from_x), (stage_y, from_y), (stage_z, from_z))):
        copies = []
        for i, peer in enumerate(stage):
            copy = pltpu.make_async_remote_copy(
                src_ref=tile.at[k], dst_ref=landing.at[i], send_sem=ss.at[base + i],
                recv_sem=rs.at[base + i], device_id=peer, device_id_type=MESH,
            )
            copy.start()
            copies.append(copy)
        base += len(stage)
        sent += copies
        for copy in copies:
            copy.wait_recv()
        table = tile[k]
        for i in range(len(stage)):
            table = jnp.maximum(table, landing[i])
        tile[k + 1] = table

    level_of = lax.shift_right_logical(table, 8).astype(F32)
    length_of = jnp.bitwise_and(table, 255).astype(F32)

    def largest(v):
        return jnp.max(jnp.max(v, axis=1, keepdims=True), axis=0, keepdims=True)

    active = jnp.zeros((1, 1), F32)
    inbound = jnp.zeros((1, 1), F32)
    arriving = jnp.zeros((1, 1), F32)
    for level in range(LEVELS):
        here = level_of == level + 1.0
        active += largest(jnp.where(here, 1.0, 0.0)) * (1 << level)
        mine = here & (slot == flipped(rank, 1 << level) * 4 + pair)
        inbound += largest(jnp.where(mine, level + 1.0, 0.0))
        arriving += largest(jnp.where(mine, length_of, 0.0))
    third = jnp.where(inbound > 0.0, arriving, jnp.full((1, 1), lengths[2], jnp.int32).astype(F32))
    branch = jnp.full((1, 1), float(len(PAIRS)), F32)
    way = jnp.ones((1, 1), F32)
    for p, (a, b) in enumerate(PAIRS):
        sets = [(1 << a) + (1 << b)] + [1 << s for s, both in ALONE.items() if both == (a, b)]
        hit = active == float(sets[0])
        for other in sets[1:] + ([0] if p == 0 else []):
            hit = hit | (active == float(other))
        branch = jnp.where(hit, float(p), branch)
        by = jnp.where(inbound == a + 1.0, 1.0, jnp.where(inbound == b + 1.0, 2.0, 0.0))
        way = jnp.where(hit, by, way)
    row = lax.broadcasted_iota(jnp.int32, shape, 0)
    told = jnp.zeros(shape, F32)
    for i, v in enumerate((branch, way, third, inbound, active)):
        told = jnp.where(row == i, v, told)
    info[...] = told.astype(jnp.int32)
    for copy in sent:
        copy.wait_send()


def plan(destination, lengths):
    vmem = pltpu.VMEM
    t = (8, 128)
    n = 2 * NX - 1 + NY - 1 + NZ - 1
    return pl.pallas_call(
        plan_kernel,
        out_shape=jax.ShapeDtypeStruct(t, jnp.int32),
        in_specs=[pl.BlockSpec(memory_space=pltpu.SMEM)] * 2,
        out_specs=pl.BlockSpec(memory_space=vmem),
        scratch_shapes=[
            vmem((4,) + t, jnp.int32),
            vmem((2 * NX - 1,) + t, jnp.int32),
            vmem((NY - 1,) + t, jnp.int32),
            vmem((NZ - 1,) + t, jnp.int32),
            pltpu.SemaphoreType.DMA((n,)),
            pltpu.SemaphoreType.DMA((n,)),
        ],
        compiler_params=pltpu.CompilerParams(collective_id=2, has_side_effects=True),
        name="plan",
    )(destination, lengths)


def move_pair(p):
    peers_of = PAIRS[p]

    def kernel(tokens, cotangent, tok_a, cot_a, tok_b, cot_b, ss, rs):
        peers = [across(level) for level in peers_of]
        barrier = pltpu.get_barrier_semaphore()
        for peer in peers:
            pl.semaphore_signal(barrier, inc=1, device_id=peer, device_id_type=MESH)
        pl.semaphore_wait(barrier, 2)
        copies = []
        for i, (src, dst, peer) in enumerate((
            (tokens, tok_a, peers[0]), (tokens, tok_b, peers[1]),
            (cotangent, cot_a, peers[0]), (cotangent, cot_b, peers[1]),
        )):
            copies.append(pltpu.make_async_remote_copy(
                src_ref=src.at[3], dst_ref=dst, send_sem=ss.at[i], recv_sem=rs.at[i],
                device_id=peer, device_id_type=MESH,
            ))
            copies[-1].start()
        for copy in copies:
            copy.wait()

    def call(tokens, cotangent, info):
        block = jax.ShapeDtypeStruct(tokens.shape[1:], BF16)
        upstream = jax.ShapeDtypeStruct(cotangent.shape[1:], BF16)
        return pl.pallas_call(
            kernel,
            out_shape=(block, upstream, block, upstream),
            in_specs=[pl.BlockSpec(memory_space=pl.ANY)] * 2,
            out_specs=[pl.BlockSpec(memory_space=pl.ANY)] * 4,
            scratch_shapes=[pltpu.SemaphoreType.DMA((4,)), pltpu.SemaphoreType.DMA((4,))],
            compiler_params=pltpu.CompilerParams(collective_id=3 + p, has_side_effects=True),
            name="move",
        )(tokens, cotangent)

    return call


def swapped(value, axis, apart):
    mask = 2**apart
    pairs = [(source, source ^ mask) for source in range(lax.axis_size(axis))]
    return lax.ppermute(value, axis, pairs)


def move_many(tokens, cotangent, info):
    kept = (tokens[2], cotangent[2])
    for level in range(LEVELS):

        def trade(kept, level=level):
            got = swapped((tokens[3], cotangent[3]), DP, level)
            arrived = info[3, 0] == level + 1
            return jax.tree.map(lambda new, old: jnp.where(arrived, new, old), got, kept)

        needed = jnp.bitwise_and(jnp.right_shift(info[4, 0], level), 1) == 1
        kept = lax.cond(needed, trade, lambda kept: kept, kept)
    return (*kept, *kept)


def shards(tokens, cotangent, projection, block_lengths, destination):
    lengths = block_lengths[0]
    info = plan(destination, lengths)
    branches = [move_pair(p) for p in range(len(PAIRS))] + [move_many]
    moved = lax.switch(info[0, 0], branches, tokens, cotangent, info)
    soft = soft_signs(lengths, info, tokens, cotangent, moved, projection)
    summed = vote_sum(soft.reshape(GROUPS, 8, 2, 4, 2, 16, HS))
    return summed.transpose(1, 0, 2).reshape(8, GROUPS * HS)


def solution(mesh):
    split = Mesh(mesh.devices.reshape(8, 2, 4, 2, 2), DP_REP)
    placed = (P(DP_REP, None, None), P(DP_REP, None, None), P(), P(DP_REP, None), P(DP_REP))
    return jax.shard_map(
        shards, mesh=split, in_specs=placed, out_specs=P(DP_REP, None), check_vma=False
    )
```

profile of v0, /device:TPU:1, one launch (start us, length us, event | category | flops | bytes accessed | tf_op | source)
XLA Modules:
  0.0 120.7 jit_solution(1420086156372835685)
XLA Ops:
  0.7 21.3 %plan.1.info = s32[8,128]{1,0:T(8,128)S(1)} custom-call(s32[1]{0:T(128)S(6)} %copy.95.dest, s32[4]{0:T(128)} %bitcast.48), custom_call_target="tpu_custom_call" | custom-call | tf_op jit(solution)/shard_map/plan/pallas_call | solution.py:503
  22.0 0.5 slice.71
  23.1 38.1 %conditional.7 = ((bf16[128,2048]{1,0:T(8,128)(2,1)}, bf16[128,1024]{1,0:T(8,128)(2,1)}, bf16[128,2048]{1,0:T(8,128)(2,1)S(1)}, bf16[128,1024]{1,0:T(8,128)(2,1)S(1)})) conditional(s32[]{:T(128)} %bitcast.27, (bf16[4,128,2048]{2,1,0:T(8,128)(2,1)}, bf16[4,128,1024]{2,1,0:T(8,128)(2,1)}) %tuple.91, ...), branch_computations={%region_0.0_spmd, %region_1.0_spmd, %region_2.0_spmd, %region_3.0_... | conditional | flops 2359326 | bytes 45614328 | solution.py:583
  23.2 37.8 %move.26 = (bf16[128,2048]{1,0:T(8,128)(2,1)}, bf16[128,1024]{1,0:T(8,128)(2,1)}, bf16[128,2048]{1,0:T(8,128)(2,1)S(1)}, bf16[128,1024]{1,0:T(8,128)(2,1)S(1)}) custom-call(bf16[4,128,2048]{2,1,0:T(8,128)(2,1)} %get-tuple-element.177.tokens, bf16[4,128,1024]{2,1,0:T(8,128)(2,1)} %get-tuple-element.178.cotangent), custom_call_target="tpu_custom_call" | custom-call | tf_op jit(solution)/shard_map/cond/branch_11_fun/move/pallas_call | solution.py:546
  61.2 21.8 %soft_signs.1 = bf16[6,2048,256]{2,1,0:T(8,128)(2,1)} custom-call(s32[4]{0:T(128)} %bitcast.49, s32[8,128]{1,0:T(8,128)S(1)} %plan.1.info, bf16[4,128,2048]{2,1,0:T(8,128)(2,1)} %tok.1, bf16[4,128,1024]{2,1,0:T(8,128)(2,1)} %cot.1, bf16[128,2048]{1,0:T(8,128)(2,1)} %get-tuple-element.234.tok_a, bf16[128,1024]{1,0:T(8,128)(2,1)} %get-tuple-element.235.cot_a, ...), custom_call_target="tpu_custom_call" | custom-call | tf_op jit(solution)/shard_map/soft_signs/pallas_call | solution.py:114
  83.0 0.0 copy-start
  83.0 2.8 %copy-done = bf16[6,2048,256]{2,1,0:T(8,128)(2,1)S(1)} copy-done((bf16[6,2048,256]{2,1,0:T(8,128)(2,1)S(1)}, bf16[6,2048,256]{2,1,0:T(8,128)(2,1)}, u32[]{:S(2)}) %copy-start) | copy-done | bytes 6291480
  85.8 34.3 %vote_sum.1 = f32[6,8,256]{2,1,0:T(8,128)S(1)} custom-call(bf16[6,8,2,4,2,16,256]{6,5,4,3,2,1,0:T(8,128)(2,1)S(1)} %bitcast.46), custom_call_target="tpu_custom_call" | custom-call | tf_op jit(solution)/shard_map/vote_sum/pallas_call | solution.py:384
  120.1 0.6 copy.96
Async XLA Ops:
  83.0 2.8 %copy-start = (bf16[6,2048,256]{2,1,0:T(8,128)(2,1)S(1)}, bf16[6,2048,256]{2,1,0:T(8,128)(2,1)}, u32[]{:S(2)}) copy-start(bf16[6,2048,256]{2,1,0:T(8,128)(2,1)} %soft_signs.1) | copy-start | bytes 18874372
where the time goes:
time: 120 us; the launch traced here: 121 us
  Pallas kernels  115 us (96%)
  local copies, waits for them, and re-layouts  3.92 us (3%)
  between operations  1.33 us (1%)
    pallas_call x1, Pallas kernels, call(): pl.pallas_call(kernel, out_shape=(block, upstream, block, upstream), in_s...  37.8 us
    pallas_call x1, Pallas kernels, vote_sum(): pl.pallas_call(vote_kernel, out_shape=jax.ShapeDtypeStruct((GROUPS, 8, HS...  34.3 us
    pallas_call x1, Pallas kernels, soft_signs(): pl.pallas_call(gradient_kernel, out_shape=jax.ShapeDtypeStruct((GROUPS, D...  21.8 us
    pallas_call x1, Pallas kernels, plan(): pl.pallas_call(plan_kernel, out_shape=jax.ShapeDtypeStruct(t, jnp.int32),...  21.3 us
    unnamed x3, local copies, waits for them, and re-layouts  3.41 us

commit v1 on v0

--- a/solution.py
+++ b/solution.py
@@ -25,119 +25,49 @@
     return lax.dot_general(a, b, (((ca,), (cb,)), ((), ())), preferred_element_type=F32)
 
 
-def gradient_kernel(
-    lengths, info, tok, cot, tok_a, cot_a, tok_b, cot_b, proj, soft, x, up, joined, comb, xt, grad
-):
-    rows = 3 * BLOCK
-    way = info[1, 0]
-
-    def chosen(own, a, b):
-        return jnp.where(way == 1, a, jnp.where(way == 2, b, own))
-
-    x[0 : 2 * BLOCK, :] = tok[0:2].reshape(2 * BLOCK, D)
-    x[2 * BLOCK : rows, :] = chosen(tok[2], tok_a[...], tok_b[...])
-    up[0 : 2 * BLOCK, :] = cot[0:2].reshape(2 * BLOCK, HEADS * HS)
-    up[2 * BLOCK : rows, :] = chosen(cot[2], cot_a[...], cot_b[...])
-
-    @pl.loop(0, GROUPS)
+def attention(at, length, joined, up, comb):
+    scale = HS ** (-0.5)
+
+    def heads(ref):
+        return jnp.concatenate([ref[at, h * HS : (h + 1) * HS] for h in range(HEADS)], axis=0)
+
+    query = heads(joined)
+    keys = joined[at, HEADS * HS : (HEADS + 1) * HS]
+    values = joined[at, (HEADS + 1) * HS :]
+    shape = (HEADS * BLOCK, BLOCK)
+    row = lax.rem(lax.broadcasted_iota(jnp.int32, shape, 0), BLOCK)
+    col = lax.broadcasted_iota(jnp.int32, shape, 1)
+    allowed = (col <= row) & (col < length)
+    scores = jnp.where(allowed, dot(query, keys, 1, 1) * scale, -1e30)
+    peak = jnp.max(scores, axis=-1, keepdims=True)
+    expo = jnp.exp(scores - peak)
+    weights = expo / jnp.sum(expo, axis=-1, keepdims=True)
+    wide = (HEADS * BLOCK, HS)
+    live = lax.rem(lax.broadcasted_iota(jnp.int32, wide, 0), BLOCK) < length
+    upstream = jnp.where(live, heads(up).astype(F32), 0.0).astype(BF16)
+    probs = weights.astype(BF16)
+    grad_values = dot(probs.T, upstream, 1, 0).astype(BF16)
+    grad_probs = dot(upstream, values, 1, 1)
+    centre = jnp.sum(weights * grad_probs, axis=-1, keepdims=True)
+    grad_scores = (weights * (grad_probs - centre) * scale).astype(BF16)
+    grad_query = dot(grad_scores, keys, 1, 0).astype(BF16)
+    grad_keys = dot(grad_scores.T, query, 1, 0).astype(BF16)
+    for h in range(HEADS):
+        comb[at, h * HS : (h + 1) * HS] = grad_query[h * BLOCK : (h + 1) * BLOCK]
+    comb[at, HEADS * HS : (HEADS + 1) * HS] = grad_keys
+    comb[at, (HEADS + 1) * HS :] = grad_values
+
+
+def columns(ref, g):
+    return ref.at[:, pl.ds(pl.multiple_of(g * HS, HS), HS)]
+
+
+def join(first, last, proj, proj_v, sem, x, joined):
+    @pl.loop(first, last)
     def _(g):
+        pltpu.make_async_copy(columns(proj, g), proj_v.at[g], sem.at[g]).wait()
         cols = pl.ds(pl.multiple_of(g * HS, HS), HS)
-        joined[:, cols] = dot(x[...], proj[:, cols], 1, 0).astype(BF16)
-
-    @pl.loop(0, D // 256)
-    def _(r):
-        at = pl.ds(pl.multiple_of(r * 256, 256), 256)
-        xt[at, :] = x[:, at].T
-
-    scale = HS ** (-0.5)
-
-    @pl.loop(0, 3)
-    def _(b):
-        at = pl.ds(pl.multiple_of(b * BLOCK, BLOCK), BLOCK)
-        length = jnp.where(b == 2, info[2, 0], lengths[b])
-
-        def heads(ref):
-            return jnp.concatenate(
-                [ref[at, h * HS : (h + 1) * HS] for h in range(HEADS)], axis=0
-            )
-
-        query = heads(joined)
-        keys = joined[at, HEADS * HS : (HEADS + 1) * HS]
-        values = joined[at, (HEADS + 1) * HS :]
-        shape = (HEADS * BLOCK, BLOCK)
-        row = lax.rem(lax.broadcasted_iota(jnp.int32, shape, 0), BLOCK)
-        col = lax.broadcasted_iota(jnp.int32, shape, 1)
-        allowed = (col <= row) & (col < length)
-        scores = jnp.where(allowed, dot(query, keys, 1, 1) * scale, -1e30)
-        peak = jnp.max(scores, axis=-1, keepdims=True)
-        expo = jnp.exp(scores - peak)
-        weights = expo / jnp.sum(expo, axis=-1, keepdims=True)
-        wide = (HEADS * BLOCK, HS)
-        live = lax.rem(lax.broadcasted_iota(jnp.int32, wide, 0), BLOCK) < length
-        upstream = jnp.where(live, heads(up).astype(F32), 0.0).astype(BF16)
-        probs = weights.astype(BF16)
-        grad_values = dot(probs.T, upstream, 1, 0).astype(BF16)
-        grad_probs = dot(upstream, values, 1, 1)
-        centre = jnp.sum(weights * grad_probs, axis=-1, keepdims=True)
-        grad_scores = (weights * (grad_probs - centre) * scale).astype(BF16)
-        grad_query = dot(grad_scores, keys, 1, 0).astype(BF16)
-        grad_keys = dot(grad_scores.T, query, 1, 0).astype(BF16)
-        for h in range(HEADS):
-            comb[at, h * HS : (h + 1) * HS] = grad_query[h * BLOCK : (h + 1) * BLOCK]
-        comb[at, HEADS * HS : (HEADS + 1) * HS] = grad_keys
-        comb[at, (HEADS + 1) * HS :] = grad_values
-
-    tile = 256
-
-    @pl.loop(0, GROUPS)
-    def _(g):
-        cols = pl.ds(pl.multiple_of(g * HS, HS), HS)
-        total = jnp.zeros((8, HS), F32)
-        for r in range(D // tile):
-            part = dot(xt[r * tile : (r + 1) * tile, :], comb[:, cols], 1, 0)
-            grad[r * tile : (r + 1) * tile, :] = part
-            total += jnp.sum((part * part).reshape(tile // 8, 8, HS), axis=0)
-        total = jnp.sum(jnp.sum(total, axis=0, keepdims=True), axis=1, keepdims=True)
-        spread = 0.25 * jnp.sqrt(total * (1.0 / (D * HS)) + 1e-06)
-
-        @pl.loop(0, D // 128)
-        def _(r):
-            at = pl.ds(pl.multiple_of(r * 128, 128), 128)
-            part = grad[at, :]
-            soft[g, at, :] = (part / (jnp.abs(part) + spread)).astype(BF16)
-
-
-def soft_signs(lengths, info, tokens, cotangent, moved, projection):
-    vmem = pltpu.VMEM
-    rows = 3 * BLOCK
-    width = GROUPS * HS
-    return pl.pallas_call(
-        gradient_kernel,
-        out_shape=jax.ShapeDtypeStruct((GROUPS, D, HS), BF16),
-        grid=(1,),
-        in_specs=[
-            pl.BlockSpec(memory_space=pltpu.SMEM),
-            pl.BlockSpec(memory_space=pltpu.SMEM),
-            pl.BlockSpec((3, BLOCK, D), lambda i: (0, 0, 0)),
-            pl.BlockSpec((3, BLOCK, HEADS * HS), lambda i: (0, 0, 0)),
-            pl.BlockSpec((BLOCK, D), lambda i: (0, 0)),
-            pl.BlockSpec((BLOCK, HEADS * HS), lambda i: (0, 0)),
-            pl.BlockSpec((BLOCK, D), lambda i: (0, 0)),
-            pl.BlockSpec((BLOCK, HEADS * HS), lambda i: (0, 0)),
-            pl.BlockSpec((D, width), lambda i: (0, 0)),
-        ],
-        out_specs=pl.BlockSpec((GROUPS, D, HS), lambda i: (0, 0, 0)),
-        scratch_shapes=[
-            vmem((rows, D), BF16),
-            vmem((rows, HEADS * HS), BF16),
-            vmem((rows, width), BF16),
-            vmem((rows, width), BF16),
-            vmem((D, rows), BF16),
-            vmem((D, HS), F32),
-        ],
-        compiler_params=pltpu.CompilerParams(vmem_limit_bytes=60 << 20),
-        name="soft_signs",
-    )(lengths, info, tokens, cotangent, *moved, projection)
+        joined[:, cols] = dot(x[...], proj_v[g], 1, 0).astype(BF16)
 
 
 NZ, NY, NX = 8, 4, 4
@@ -147,9 +77,11 @@
     return lax.rem(i + n, n)
 
 
-def vote_kernel(soft, out, own, part, wz, wx, wy, rzp0, rzp1, rzm0, rzm1, szp0, szp1, szm0,
+def vote_kernel(lengths, info, tok, cot, tok_a, cot_a, tok_b, cot_b, proj, comb_hbm, xt_hbm, out,
+                cand_t, cand_c, proj_v, comb01, xt01, x3, up3, joined3, comb3, xt3, grad, mail,
+                part, wz, wx, wy, rzp0, rzp1, rzm0, rzm1, szp0, szp1, szm0,
                 szm1, rx, sx, ry, sy, ux, uy, uz, vx, vy, vz, tx, ty, tz, qx, qy, qz, res, fin,
-                loc, s0, r0, s1, r1, s2, r2, s3, r3, s4, r4):
+                loc, psem, s0, r0, s1, r1, s2, r2, s3, r3, s4, r4):
     z, xh, y, xl, core = [lax.axis_index(a) for a in DP_REP]
     x = xh * 2 + xl
 
@@ -163,17 +95,25 @@
         return {"dp_0": i}
 
     partner = {"rep_1": 1 - core}
+
+    loads = [(tok.at[2], cand_t.at[0]), (tok_a, cand_t.at[1]), (tok_b, cand_t.at[2])]
+    loads += [(cot.at[2], cand_c.at[0]), (cot_a, cand_c.at[1]), (cot_b, cand_c.at[2])]
+    loads += [(comb_hbm, comb01), (xt_hbm, xt01)]
+    loads = [pltpu.make_async_copy(a, b, loc.at[i]) for i, (a, b) in enumerate(loads)]
+    for load in loads[:3]:
+        load.start()
+    for g in range(GROUPS):
+        pltpu.make_async_copy(columns(proj, g), proj_v.at[g], psem.at[g]).start()
+    for load in loads[3:]:
+        load.start()
 
     barrier = pltpu.get_barrier_semaphore()
     peers = [partner]
     peers += [at_x(wrap(x + d, NX)) for d in range(1, NX)]
     peers += [at_y(wrap(y + d, NY)) for d in range(1, NY)]
     peers += [at_z(wrap(z + d, NZ)) for d in range(1, NZ)]
-    for j in range(3):
-        pltpu.make_async_copy(soft.at[core * 3 + j], own.at[j], loc.at[j]).start()
     for peer in peers:
         pl.semaphore_signal(barrier, inc=1, device_id=peer, device_id_type=MESH)
-    pl.semaphore_wait(barrier, len(peers))
 
     sent = []
 
@@ -185,27 +125,80 @@
         sent.append(copy)
         return copy
 
-    first = [
-        send(soft.at[(1 - core) * 3 + j], part.at[j], s0.at[j], r0.at[j], partner)
-        for j in range(3)
-    ]
-
     def add(*refs):
         total = refs[0][...].astype(F32)
         for ref in refs[1:]:
             total = total + ref[...].astype(F32)
         return total
 
-    def arrive(j):
-        pltpu.make_async_copy(soft.at[core * 3 + j], own.at[j], loc.at[j]).wait()
-        first[j].wait_recv()
-
-    arrive(0)
-
-    @pl.loop(0, NZ)
-    def _(a):
-        for h in range(2):
-            wz[a, h] = add(own.at[0, a, h], part.at[0, a, h]).astype(BF16)
+    way = info[1, 0]
+
+    def chosen(c):
+        return jnp.where(way == 1, c[1], jnp.where(way == 2, c[2], c[0]))
+
+    for load in loads[:3]:
+        load.wait()
+    x3[...] = chosen(cand_t)
+    join(0, GROUPS, proj, proj_v, psem, x3, joined3)
+    for r in range(D // 512):
+        xt3[r * 512 : (r + 1) * 512, :] = x3[:, r * 512 : (r + 1) * 512].T
+    for load in loads[3:]:
+        load.wait()
+    up3[...] = chosen(cand_c)
+    attention(slice(None), info[2, 0], joined3, up3, comb3)
+    pl.semaphore_wait(barrier, len(peers))
+
+    tile = 128
+    other = 1 - core
+
+    def step(begin, end):
+        if begin is not None:
+            j, to_partner, buf = begin
+            cols = pl.ds(pl.multiple_of(((other if to_partner else core) * 3 + j) * HS, HS), HS)
+
+        def body(a, total):
+            for h in range(2):
+                at = pl.ds(pl.multiple_of(a * 256 + h * tile, tile), tile)
+                if begin is not None:
+                    new = dot(xt01[at, :], comb01[:, cols], 1, 0)
+                    new = new + dot(xt3[at, :], comb3[:, cols], 1, 0)
+                    grad[buf, at, :] = new
+                    total = total + jnp.sum((new * new).reshape(tile // 8, 8, HS), axis=0)
+                if end is not None:
+                    old = grad[end[2], at, :]
+                    soft = (old / (jnp.abs(old) + end[3])).reshape(NY, 2, 16, HS)
+                    if end[1]:
+                        mail[end[0], a, h] = soft.astype(BF16)
+                    else:
+                        both = (soft + part[end[0], a, h].astype(F32)).astype(BF16)
+                        if end[0] == 0:
+                            wz[a, h] = both
+                        elif end[0] == 1:
+                            for l in range(2):
+                                wx[h, l, a] = both[:, l]
+                        else:
+                            for b in range(NY):
+                                wy[b, a, h] = both[b]
+            return total
+
+        total = lax.fori_loop(0, NZ, body, jnp.zeros((8, HS), F32))
+        if begin is None:
+            return None
+        total = jnp.sum(jnp.sum(total, axis=0, keepdims=True), axis=1, keepdims=True)
+        return (*begin, 0.25 * jnp.sqrt(total * (1.0 / (D * HS)) + 1e-06))
+
+    first = {}
+
+    def post(j):
+        first[j] = send(mail.at[j], part.at[j], s0.at[j], r0.at[j], partner)
+
+    now = step((0, True, 0), None)
+    now = step((1, True, 1), now)
+    post(0)
+    now = step((0, False, 0), now)
+    post(1)
+    first[0].wait_recv()
+    now = step((2, True, 1), now)
 
     up_z, down_z = at_z(wrap(z + 1, NZ)), at_z(wrap(z - 1, NZ))
 
@@ -247,22 +240,13 @@
     wx_of = lambda c: wx.at[lax.div(c, 2), lax.rem(c, 2)]
     wy_of = lambda c: wy.at[c]
 
-    arrive(1)
-
-    @pl.loop(0, NZ)
-    def _(a):
-        for h in range(2):
-            for l in range(2):
-                wx[h, l, a] = add(own.at[1, a, h, :, l], part.at[1, a, h, :, l]).astype(BF16)
-
+    now = step((1, False, 0), now)
+    post(2)
+    first[1].wait_recv()
+    now = step((2, False, 1), now)
     bx = four_ring(1, x, wx_of, at_x, rx, 0)
-    arrive(2)
-
-    @pl.loop(0, NZ)
-    def _(a):
-        for b in range(NY):
-            wy[b, a] = add(own.at[2, a, :, b], part.at[2, a, :, b]).astype(BF16)
-
+    first[2].wait_recv()
+    step(None, now)
     by = four_ring(2, y, wy_of, at_y, ry, 6)
 
     def z_relay(k):
@@ -357,12 +341,23 @@
         copy.wait_send()
 
 
-def vote_sum(soft):
+def vote_sum(lengths, info, tokens, cotangent, moved, projection, comb, xt):
     vmem = pltpu.VMEM
     t = (16, HS)
     bf = lambda *dims: vmem(dims + t, BF16)
     sems = lambda n: pltpu.SemaphoreType.DMA((n,))
     scratch = [
+        vmem((3, BLOCK, D), BF16),
+        vmem((3, BLOCK, HEADS * HS), BF16),
+        vmem((GROUPS, D, HS), BF16),
+        vmem((2 * BLOCK, GROUPS * HS), BF16),
+        vmem((D, 2 * BLOCK), BF16),
+        vmem((BLOCK, D), BF16),
+        vmem((BLOCK, HEADS * HS), BF16),
+        vmem((BLOCK, GROUPS * HS), BF16),
+        vmem((BLOCK, GROUPS * HS), BF16),
+        vmem((D, BLOCK), BF16),
+        vmem((2, D, HS), F32),
         bf(3, 8, 2, 4, 2),
         bf(3, 8, 2, 4, 2),
         bf(8, 2, 4, 2),
@@ -378,20 +373,21 @@
         bf(7), bf(7), bf(3),
         vmem((3, 2, 8, HS), F32),
         vmem((3, 8, HS), F32),
-        sems(3),
+        sems(8), sems(6),
         sems(6), sems(6), sems(16), sems(16), sems(12), sems(12), sems(9), sems(9), sems(17), sems(17),
     ]
     return pl.pallas_call(
         vote_kernel,
         out_shape=jax.ShapeDtypeStruct((GROUPS, 8, HS), F32),
-        in_specs=[pl.BlockSpec(memory_space=pl.ANY)],
+        in_specs=[pl.BlockSpec(memory_space=pltpu.SMEM)] * 2
+        + [pl.BlockSpec(memory_space=pltpu.HBM)] * 9,
         out_specs=pl.BlockSpec(memory_space=pltpu.VMEM),
         scratch_shapes=scratch,
         compiler_params=pltpu.CompilerParams(
             collective_id=1, has_side_effects=True, vmem_limit_bytes=40 << 20
         ),
         name="vote_sum",
-    )(soft)
+    )(lengths, info, tokens, cotangent, *moved, projection, comb, xt)
 
 
 LEVELS = 6
@@ -411,7 +407,8 @@
     return {"dp_0": flipped(lax.axis_index("dp_0"), 1 << (level - 3))}
 
 
-def plan_kernel(dest, lengths, info, tile, from_x, from_y, from_z, ss, rs):
+def plan_kernel(dest, lengths, tok, cot, proj, info, comb, xt, x01, up01, proj_v, joined, tile,
+                from_x, from_y, from_z, loc, psem, ss, rs):
     z, xh, y, xl, core = [lax.axis_index(a) for a in DP_REP]
     x = xh * 2 + xl
     rank = (z * 2 + xh) * 4 + y
@@ -426,6 +423,18 @@
     stage_y = [{"dp_2": wrap(y + d, NY)} for d in range(1, NY)]
     stage_z = [{"dp_0": wrap(z + d, NZ)} for d in range(1, NZ)]
     peers = stage_x + stage_y + stage_z
+
+    halves = [pl.ds(0, BLOCK), pl.ds(BLOCK, BLOCK)]
+    loads = [(tok.at[b], x01.at[halves[b]]) for b in range(2)]
+    loads += [(cot.at[b], up01.at[halves[b]]) for b in range(2)]
+    loads = [pltpu.make_async_copy(a, b, loc.at[i]) for i, (a, b) in enumerate(loads)]
+    for load in loads[:2]:
+        load.start()
+    for g in range(GROUPS):
+        pltpu.make_async_copy(columns(proj, g), proj_v.at[g], psem.at[g]).start()
+    for load in loads[2:]:
+        load.start()
+
     barrier = pltpu.get_barrier_semaphore()
     for peer in peers:
         pl.semaphore_signal(barrier, inc=1, device_id=peer, device_id_type=MESH)
@@ -439,6 +448,27 @@
     code = code * 256 + jnp.full(shape, lengths[3], jnp.int32)
     mine = (slot == rank * 4 + pair) & (target >= 0)
     tile[0] = jnp.where(mine, code, 0)
+
+    def before_any():
+        for load in loads[:2]:
+            load.wait()
+        join(0, 3, proj, proj_v, psem, x01, joined)
+
+    def beside_x():
+        join(3, GROUPS, proj, proj_v, psem, x01, joined)
+        for load in loads[2:]:
+            load.wait()
+
+    def beside_y():
+        attention(halves[0], lengths[0], joined, up01, comb)
+
+    def beside_z():
+        attention(halves[1], lengths[1], joined, up01, comb)
+        for r in range(D // 256):
+            xt[r * 256 : (r + 1) * 256, :] = x01[:, r * 256 : (r + 1) * 256].T
+
+    beside = (beside_x, beside_y, beside_z)
+    before_any()
     pl.semaphore_wait(barrier, len(peers))
 
     sent = []
@@ -454,6 +484,7 @@
             copies.append(copy)
         base += len(stage)
         sent += copies
+        beside[k]()
         for copy in copies:
             copy.wait_recv()
         table = tile[k]
@@ -496,26 +527,39 @@
         copy.wait_send()
 
 
-def plan(destination, lengths):
+def plan(destination, lengths, tokens, cotangent, projection):
     vmem = pltpu.VMEM
     t = (8, 128)
     n = 2 * NX - 1 + NY - 1 + NZ - 1
     return pl.pallas_call(
         plan_kernel,
-        out_shape=jax.ShapeDtypeStruct(t, jnp.int32),
-        in_specs=[pl.BlockSpec(memory_space=pltpu.SMEM)] * 2,
-        out_specs=pl.BlockSpec(memory_space=vmem),
+        out_shape=(
+            jax.ShapeDtypeStruct(t, jnp.int32),
+            jax.ShapeDtypeStruct((2 * BLOCK, GROUPS * HS), BF16),
+            jax.ShapeDtypeStruct((D, 2 * BLOCK), BF16),
+        ),
+        in_specs=[pl.BlockSpec(memory_space=pltpu.SMEM)] * 2
+        + [pl.BlockSpec(memory_space=pltpu.HBM)] * 3,
+        out_specs=[pl.BlockSpec(memory_space=vmem)] * 3,
         scratch_shapes=[
+            vmem((2 * BLOCK, D), BF16),
+            vmem((2 * BLOCK, HEADS * HS), BF16),
+            vmem((GROUPS, D, HS), BF16),
+            vmem((2 * BLOCK, GROUPS * HS), BF16),
             vmem((4,) + t, jnp.int32),
             vmem((2 * NX - 1,) + t, jnp.int32),
             vmem((NY - 1,) + t, jnp.int32),
             vmem((NZ - 1,) + t, jnp.int32),
+            pltpu.SemaphoreType.DMA((4,)),
+            pltpu.SemaphoreType.DMA((GROUPS,)),
             pltpu.SemaphoreType.DMA((n,)),
             pltpu.SemaphoreType.DMA((n,)),
         ],
-        compiler_params=pltpu.CompilerParams(collective_id=2, has_side_effects=True),
+        compiler_params=pltpu.CompilerParams(
+            collective_id=2, has_side_effects=True, vmem_limit_bytes=30 << 20
+        ),
         name="plan",
-    )(destination, lengths)
+    )(destination, lengths, tokens, cotangent, projection)
 
 
 def move_pair(p):
@@ -578,11 +622,10 @@
 
 def shards(tokens, cotangent, projection, block_lengths, destination):
     lengths = block_lengths[0]
-    info = plan(destination, lengths)
+    info, comb, xt = plan(destination, lengths, tokens, cotangent, projection)
     branches = [move_pair(p) for p in range(len(PAIRS))] + [move_many]
     moved = lax.switch(info[0, 0], branches, tokens, cotangent, info)
-    soft = soft_signs(lengths, info, tokens, cotangent, moved, projection)
-    summed = vote_sum(soft.reshape(GROUPS, 8, 2, 4, 2, 16, HS))
+    summed = vote_sum(lengths, info, tokens, cotangent, moved, projection, comb, xt)
     return summed.transpose(1, 0, 2).reshape(8, GROUPS * HS)
 
 

time: 120 us -> 114 us (0.950)
  Pallas kernels: 115 us -> 105 us
  local copies, waits for them, and re-layouts: 3.92 us -> 7.36 us
    pallas_call x2 -> x1, Pallas kernels: 43.1 us -> 21.5 us  [plan(): pl.pallas_call(plan_kernel, out_shape=(jax.ShapeDtypeStruct(t, jnp.int32)...]
    pallas_call x1, Pallas kernels: 34.3 us -> 51.5 us  [vote_sum(): pl.pallas_call(vote_kernel, out_shape=jax.ShapeDtypeStruct((GROUPS, 8, HS...]
    pallas_call x1, Pallas kernels: 37.8 us -> 32.1 us  [call(): pl.pallas_call(kernel, out_shape=(block, upstream, block, upstream), in_s...]
    unnamed x3 -> x11, local copies, waits for them, and re-layouts: 3.41 us -> 6.85 us
where the time goes in v1:
time: 114 us
  Pallas kernels  105 us (92%)
  local copies, waits for them, and re-layouts  7.36 us (6%)
  between operations  1.37 us (1%)
    pallas_call x1, Pallas kernels, vote_sum(): pl.pallas_call(vote_kernel, out_shape=jax.ShapeDtypeStruct((GROUPS, 8, HS...  51.5 us
    pallas_call x1, Pallas kernels, call(): pl.pallas_call(kernel, out_shape=(block, upstream, block, upstream), in_s...  32.1 us
    pallas_call x1, Pallas kernels, plan(): pl.pallas_call(plan_kernel, out_shape=(jax.ShapeDtypeStruct(t, jnp.int32)...  21.5 us
    unnamed x11, local copies, waits for them, and re-layouts  6.85 us

profile of v1, /device:TPU:1, one launch (start us, length us, event | category | flops | bytes accessed | tf_op | source)
XLA Modules:
  0.0 114.2 jit_solution(11585661908358861855)
XLA Ops:
  0.7 0.0 copy-start
  0.7 2.8 %copy-done = bf16[2048,1536]{1,0:T(8,128)(2,1)S(1)} copy-done((bf16[2048,1536]{1,0:T(8,128)(2,1)S(1)}, bf16[2048,1536]{1,0:T(8,128)(2,1)}, u32[]{:S(2)}) %copy-start) | copy-done | bytes 6291480
  3.4 0.0 copy-start.2
  3.4 0.7 copy-done.2
  4.1 0.0 copy-start.4
  4.1 21.5 %plan.1 = (s32[8,128]{1,0:T(8,128)S(1)}, bf16[256,1536]{1,0:T(8,128)(2,1)S(1)}, bf16[2048,256]{1,0:T(8,128)(2,1)S(1)}) custom-call(s32[1]{0:T(128)S(6)} %copy.95.dest, s32[4]{0:T(128)S(1)} %bitcast.46, bf16[4,128,2048]{2,1,0:T(8,128)(2,1)} %tok.3, bf16[4,128,1024]{2,1,0:T(8,128)(2,1)} %cot.3, bf16[2048,1536]{1,0:T(8,128)(2,1)S(1)} %copy-done), custom_call_target="tpu_custom_call" | custom-call | tf_op jit(solution)/shard_map/plan/pallas_call | solution.py:534
  25.6 0.5 slice.71
  26.8 0.0 copy-done.4
  26.8 0.0 copy-start.3
  26.8 32.4 %conditional.7 = ((bf16[128,2048]{1,0:T(8,128)(2,1)}, bf16[128,1024]{1,0:T(8,128)(2,1)}, bf16[128,2048]{1,0:T(8,128)(2,1)S(1)}, bf16[128,1024]{1,0:T(8,128)(2,1)})) conditional(s32[]{:T(128)} %bitcast.27, (bf16[4,128,2048]{2,1,0:T(8,128)(2,1)}, bf16[4,128,1024]{2,1,0:T(8,128)(2,1)S(1)}) %tuple.149, ...), branch_computations={%region_0.0_spmd, %region_1.0_spmd, %region_2.0_spmd, %region_3.0_... | conditional | flops 2359326 | bytes 45614328 | solution.py:627
  26.8 32.1 %move.19 = (bf16[128,2048]{1,0:T(8,128)(2,1)}, bf16[128,1024]{1,0:T(8,128)(2,1)}, bf16[128,2048]{1,0:T(8,128)(2,1)S(1)}, bf16[128,1024]{1,0:T(8,128)(2,1)}) custom-call(bf16[4,128,2048]{2,1,0:T(8,128)(2,1)} %get-tuple-element.163.tokens, bf16[4,128,1024]{2,1,0:T(8,128)(2,1)S(1)} %get-tuple-element.164.cotangent), custom_call_target="tpu_custom_call" | custom-call | tf_op jit(solution)/shard_map/cond/branch_4_fun/move/pallas_call | solution.py:590
  59.2 0.0 copy-done.3
  59.2 0.0 copy-start.1
  59.2 2.8 %copy-done.1 = bf16[2048,1536]{1,0:T(8,128)(2,1)S(1)} copy-done((bf16[2048,1536]{1,0:T(8,128)(2,1)S(1)}, bf16[2048,1536]{1,0:T(8,128)(2,1)}, u32[]{:S(2)}) %copy-start.1) | copy-done | bytes 6291480
  62.0 51.5 %vote_sum.1 = f32[6,8,256]{2,1,0:T(8,128)S(1)} custom-call(s32[4]{0:T(128)S(1)} %bitcast.47, s32[8,128]{1,0:T(8,128)S(1)} %get-tuple-element.237.info, bf16[4,128,2048]{2,1,0:T(8,128)(2,1)} %tok.3, bf16[4,128,1024]{2,1,0:T(8,128)(2,1)S(1)} %copy-done.4, bf16[128,2048]{1,0:T(8,128)(2,1)} %get-tuple-element.238.tok_a, ...), custom_call_target="tpu_custom_call" | custom-call | tf_op jit(solution)/shard_map/vote_sum/pallas_call | solution.py:379
  113.5 0.6 copy.96
Async XLA Ops:
  0.7 2.8 %copy-start = (bf16[2048,1536]{1,0:T(8,128)(2,1)S(1)}, bf16[2048,1536]{1,0:T(8,128)(2,1)}, u32[]{:S(2)}) copy-start(bf16[2048,1536]{1,0:T(8,128)(2,1)} %proj.3) | copy-start | bytes 18874372
  3.4 0.7 copy-start.2
  4.1 22.7 %copy-start.4 = (bf16[4,128,1024]{2,1,0:T(8,128)(2,1)S(1)}, bf16[4,128,1024]{2,1,0:T(8,128)(2,1)}, u32[]{:S(2)}) copy-start(bf16[4,128,1024]{2,1,0:T(8,128)(2,1)} %cot.3) | copy-start | bytes 3145732
  26.8 32.4 %copy-start.3 = (s32[1,4]{1,0:T(1,128)S(1)}, s32[1,4]{1,0:T(1,128)}, u32[]{:S(2)}) copy-start(s32[1,4]{1,0:T(1,128)} %param.36) | copy-start | bytes 52
  59.2 2.8 %copy-start.1 = (bf16[2048,1536]{1,0:T(8,128)(2,1)S(1)}, bf16[2048,1536]{1,0:T(8,128)(2,1)}, u32[]{:S(2)}) copy-start(bf16[2048,1536]{1,0:T(8,128)(2,1)} %proj.3) | copy-start | bytes 18874372
